TPU v7x, 8 devices: a whole 2x2x1 slice. The times are simulated.
8 devices in a mesh: dp: 1 (over z), tp: 8 (over x, y, core).
Axes of the slice: x: 2, y: 2, z: 1, core: 2. Of those that a mesh axis runs over, the one named last changes fastest.
Arguments:
- x: bfloat16 [2048, 7168], P('dp')
- w_gate: bfloat16 [7168, 18432], P(None, 'tp')
- w_up: bfloat16 [7168, 18432], P(None, 'tp')
- w_down: bfloat16 [18432, 7168], P('tp')
Outputs:
- output: bfloat16 [2048, 7168], P('dp')
All inputs are finite; a program needn't handle non-finite values.
Results may differ from a plain program's by a relative error of at most 0.016.
Values are sent between devices in bfloat16 or wider.
A program may use at most 2 GiB of HBM per device.

v0:
```python
import jax
import jax.numpy as jnp
from jax import lax
from jax.sharding import PartitionSpec as P


def solution(mesh):
    def step(x, w_gate, w_up, w_down):
        gate = jnp.dot(x, w_gate, preferred_element_type=jnp.float32)
        up = jnp.dot(x, w_up, preferred_element_type=jnp.float32)
        hidden = (jax.nn.silu(gate) * up).astype(jnp.bfloat16)
        term = jnp.dot(hidden, w_down, preferred_element_type=jnp.float32).astype(jnp.bfloat16)
        return lax.psum(term, "tp")

    return jax.shard_map(
        step,
        mesh=mesh,
        in_specs=(P("dp", None), P(None, "tp"), P(None, "tp"), P("tp", None)),
        out_specs=P("dp", None),
        check_vma=False,
    )
```

profile of v0, /device:TPU:0, one launch (start us, length us, event | category | flops | bytes accessed | tf_op | source)
XLA Modules:
  0.0 616.7 jit_solution(8534373869698612612)
XLA Ops:
  6.5 0.0 all-reduce.2.cloned.1.call-start
  6.5 78.2 %fusion = f32[2048,2304]{1,0:T(8,128)} fusion(bf16[2048,7168]{1,0:T(8,128)(2,1)} %param.4, bf16[7168,2304]{1,0:T(8,128)(2,1)} %param.5), kind=kOutput, calls=%fused_computation.2 | convolution fusion | flops 67645734912 | bytes 81264640 | tf_op jit(solution)/shard_map/dot_general | solution.py:9
  84.7 84.3 %multiply_convert_fusion = bf16[2048,2304]{1,0:T(8,128)(2,1)} fusion(f32[2048,2304]{1,0:T(8,128)} %fusion, bf16[2048,7168]{1,0:T(8,128)(2,1)} %param.4, bf16[7168,2304]{1,0:T(8,128)(2,1)} %param.6), kind=kOutput, calls=%fused_computation.1 | convolution fusion | flops 67674046464 | bytes 90701824 | tf_op jit(solution)/shard_map/dot_general | solution.py:10
  169.0 77.1 %convolution_convert_fusion = bf16[2048,7168]{1,0:T(8,128)(2,1)} fusion(bf16[2048,2304]{1,0:T(8,128)(2,1)} %multiply_convert_fusion, bf16[2304,7168]{1,0:T(8,128)(2,1)} %param.7), kind=kOutput, calls=%fused_computation | convolution fusion | flops 67660414976 | bytes 71827456 | tf_op jit(solution)/shard_map/dot_general | solution.py:12
  246.1 0.0 all-reduce.2.cloned.1.call-update
  246.1 343.6 %all-reduce.2.cloned.1.call-done = bf16[2048,7168]{1,0:T(8,128)(2,1)} async-done(((bf16[2048,7168]{1,0:T(8,128)(2,1)}), bf16[2048,7168]{1,0:T(8,128)(2,1)}) %all-reduce.2.cloned.1.call-update) | async-done | bytes 29360144 | tf_op jit(solution)/shard_map/psum | solution.py:13
  589.7 20.1 %copy.6 = bf16[2048,7168]{1,0:T(8,128)(2,1)} copy(bf16[2048,7168]{1,0:T(8,128)(2,1)} %all-reduce.2.cloned.1.call-done) | data formatting | bytes 58720256
Async XLA Ops:
  6.5 583.1 %all-reduce.2.cloned.1.call-start = ((), (), s32[]{:S(2)}) async-start(), calls=%async_computation | async-start | bytes 58720256 | tf_op jit(solution)/shard_map/psum | solution.py:13
Sparse Core Ops, SparseCore 0:
  246.2 343.4 all-reduce.1
where the time goes:
time: 617 us
  waiting for transfers between devices  344 us (56%)
  matrix products  240 us (39%)
  local copies, waits for them, and re-layouts  20.1 us (3%)
  between operations  13.4 us (2%)
    psum x1, waiting for transfers between devices, step(): return lax.psum(term, 'tp')  344 us
    dot_general x1, matrix products, step(): up = jnp.dot(x, w_up, preferred_element_type=jnp.float32)  84.3 us
    dot_general x1, matrix products, step(): gate = jnp.dot(x, w_gate, preferred_element_type=jnp.float32)  78.2 us
    dot_general x1, matrix products, step(): jnp.dot(hidden, w_down, preferred_element_type=jnp.float32)  77.1 us
    unnamed x1, local copies, waits for them, and re-layouts  20.1 us
  transfers between devices with their start and end apart: 1, of which 1 were waited for; matrix products, arithmetic and copies ran while one was open for 0% of the time, Pallas kernels for 0%

commit v1 on v0

v1 whole, which is shorter than its diff:
```python
import functools

import jax
import jax.numpy as jnp
from jax import lax
from jax.experimental import pallas as pl
from jax.experimental.pallas import tpu as pltpu
from jax.sharding import PartitionSpec as P

MESH = pl.DeviceIdType.MESH
BF16, F32 = jnp.bfloat16, jnp.float32
M = 256
HALF, QUARTER, EIGHTH = M // 2, M // 4, M // 8
TH = 256
W = 1024


def kernel(
    n_chunks, n_gu, n_dn,
    x_hbm, wg_hbm, wu_hbm, wd_hbm, y_hbm,
    xbuf, wbuf, acc, hbuf, wdbuf, keep, sp, rp, k1, s1, r1, k2, s2, r2, fin,
    x_sem, w_sem, wd_sem, p_send, p_recv, a_send, a_recv, b_send, b_recv,
    loc_sem, g1_send, g1_recv, g2_send, g2_recv, g3_send, g3_recv, q_send, q_recv, credit,
):
    me = lax.axis_index("tp")
    dx, dy, dc = me // 4, (me // 2) % 2, me % 2
    sib = me + 1 - 2 * dc
    depth = x_hbm.shape[1]
    kh = depth // 2
    n_tiles = n_chunks * n_gu
    n_units = n_chunks * n_dn

    def remote(src, dst, send, recv, dev):
        return pltpu.make_async_remote_copy(
            src_ref=src, dst_ref=dst, send_sem=send, recv_sem=recv, device_id={"tp": dev}, device_id_type=MESH
        )

    def w_copies(t, part):
        col = pl.multiple_of((t % n_gu) * TH, TH)
        rows = pl.ds(part * kh, kh)
        slot = t % 2
        return [
            pltpu.make_async_copy(
                src.at[rows, pl.ds(col, TH)], wbuf.at[slot, rows, pl.ds(TH * n, TH)], w_sem.at[slot, part, n]
            )
            for n, src in enumerate((wg_hbm, wu_hbm))
        ]

    def x_copies(k):
        own = pl.multiple_of(k * M + dc * HALF, HALF)
        other = pl.multiple_of(k * M + (1 - dc) * HALF, HALF)
        return [
            pltpu.make_async_copy(x_hbm.at[pl.ds(own, HALF)], xbuf.at[pl.ds(0, HALF)], x_sem.at[0]),
            pltpu.make_async_copy(x_hbm.at[pl.ds(other, HALF)], xbuf.at[pl.ds(HALF, HALF)], x_sem.at[1]),
        ]

    def wd_copy(j):
        return pltpu.make_async_copy(
            wd_hbm.at[:, pl.ds(pl.multiple_of(j * W, W), W)], wdbuf.at[j], wd_sem.at[j]
        )

    def pair_copy(j):
        return remote(sp.at[j], rp.at[j], p_send.at[j], p_recv.at[j], sib)

    def place(u):
        e = u % 2
        xa, ya = dx + (1 - e) * (1 - 2 * dx), dy + e * (1 - 2 * dy)
        xb, yb = dx + e * (1 - 2 * dx), dy + (1 - e) * (1 - 2 * dy)
        p, r = dx * (1 - e) + dy * e, dx * e + dy * (1 - e)
        return 4 * xa + 2 * ya + dc, 4 * xb + 2 * yb + dc, p, r

    def block(u, p, r):
        row = pl.multiple_of((u // n_dn) * M + dc * HALF + p * QUARTER + r * EIGHTH, EIGHTH)
        return y_hbm.at[pl.ds(row, EIGHTH), pl.ds(pl.multiple_of((u % n_dn) * W, W), W)]

    def half_block(u):
        row = pl.multiple_of((u // n_dn) * M + dc * HALF, HALF)
        return y_hbm.at[pl.ds(row, HALF), pl.ds(pl.multiple_of((u % n_dn) * W, W), W)]

    def a_copy(u):
        a, _, _, _ = place(u)
        s = u % 4
        return remote(s1.at[s], r1.at[s], a_send.at[s], a_recv.at[s], a)

    def b_copy(u):
        _, b, _, _ = place(u)
        s = u % 4
        return remote(s2.at[s], r2.at[s], b_send.at[s], b_recv.at[s], b)

    def loc_copy(u):
        _, _, p, r = place(u)
        return pltpu.make_async_copy(fin.at[u % 4], block(u, p, r), loc_sem.at[u % 4])

    def g1_copy(u):
        _, b, p, r = place(u)
        return remote(fin.at[u % 4], block(u, p, r), g1_send.at[u % 4], g1_recv.at[u % 4], b)

    def g2_copy(u):
        a, _, p, r = place(u)
        return remote(fin.at[u % 4], block(u, p, r), g2_send.at[u % 4], g2_recv.at[u % 8], a)

    def g3_copy(u):
        a, _, p, r = place(u)
        blk = block(u, p, 1 - r)
        return remote(blk, blk, g3_send.at[u % 4], g3_recv.at[u % 8], a)

    def q_copy(u):
        blk = half_block(u)
        return remote(blk, blk, q_send, q_recv, sib)

    def tick(n):
        u5, u4, u3, u2, u1 = n - 8, n - 6, n - 4, n - 2, n

        @pl.when(u5 >= 0)
        def _():
            loc_copy(u5).wait()
            g1_copy(u5).wait_send()
            g2_copy(u5).wait()
            g3_copy(u5).wait()
            q_copy(u5).start()

        @pl.when((u4 >= 0) & (u4 < n_units))
        def _():
            g1_copy(u4).wait_recv()
            g3_copy(u4).start()

        @pl.when((u3 >= 0) & (u3 < n_units))
        def _():
            b_copy(u3).wait()
            s = u3 % 4
            fin[s] = (k2[s] + r2[s].astype(F32)).astype(BF16)
            g1_copy(u3).start()
            g2_copy(u3).start()
            loc_copy(u3).start()

        @pl.when((u2 >= 0) & (u2 < n_units))
        def _():
            a_copy(u2).wait()
            s = u2 % 4
            _, _, _, r = place(u2)
            mine = pl.ds(pl.multiple_of(r * EIGHTH, EIGHTH), EIGHTH)
            theirs = pl.ds(pl.multiple_of((1 - r) * EIGHTH, EIGHTH), EIGHTH)
            s2[s] = (k1[s, theirs] + r1[s, theirs].astype(F32)).astype(BF16)
            b_copy(u2).start()
            k2[s] = k1[s, mine] + r1[s, mine].astype(F32)

        @pl.when(u1 < n_units)
        def _():
            j = u1 % n_dn
            pair_copy(j).wait()
            s = u1 % 4
            _, _, p, _ = place(u1)
            mine = pl.ds(pl.multiple_of(p * QUARTER, QUARTER), QUARTER)
            theirs = pl.ds(pl.multiple_of((1 - p) * QUARTER, QUARTER), QUARTER)
            s1[s] = (keep[j, theirs] + rp[j, theirs].astype(F32)).astype(BF16)
            a_copy(u1).start()
            k1[s] = keep[j, mine] + rp[j, mine].astype(F32)

    for c in x_copies(0):
        c.start()
    for t in range(2):
        for part in range(2):
            for c in w_copies(t, part):
                c.start()

    barrier = pltpu.get_barrier_semaphore()
    partners = (sib, 4 * (1 - dx) + 2 * dy + dc, 4 * dx + 2 * (1 - dy) + dc)
    for dev in partners:
        pl.semaphore_signal(barrier, inc=1, device_id={"tp": dev}, device_id_type=MESH)
    pl.semaphore_wait(barrier, 3)

    def chunk(k, _):
        for c in x_copies(k):
            c.wait()

        def gate_up(i, _):
            t = k * n_gu + i
            slot = t % 2

            @pl.when((k > 0) & (i % 2 == 0))
            def _():
                tick((k - 1) * n_dn + 2 + i // 2)

            for c in w_copies(t, 0):
                c.wait()
            acc[...] = jnp.dot(xbuf[:, :kh], wbuf[slot, :kh], preferred_element_type=F32)

            @pl.when(t + 2 < n_tiles)
            def _():
                for c in w_copies(t + 2, 0):
                    c.start()

            for c in w_copies(t, 1):
                c.wait()
            gu = acc[...] + jnp.dot(xbuf[:, kh:], wbuf[slot, kh:], preferred_element_type=F32)
            g, up = gu[:, :TH], gu[:, TH:]
            hbuf[:, pl.ds(pl.multiple_of(i * TH, TH), TH)] = (g * jax.nn.sigmoid(g) * up).astype(BF16)

            @pl.when(t + 2 < n_tiles)
            def _():
                for c in w_copies(t + 2, 1):
                    c.start()

            @pl.when((k == 0) & (i >= n_gu - 2))
            def _():
                wd_copy(i - (n_gu - 2)).start()

            return 0

        lax.fori_loop(0, n_gu, gate_up, 0)

        @pl.when(k + 1 < n_chunks)
        def _():
            for c in x_copies(k + 1):
                c.start()

        @pl.when(k > 0)
        def _():
            pl.semaphore_signal(credit, inc=1, device_id={"tp": sib}, device_id_type=MESH)
            pl.semaphore_wait(credit, 1)

        def down(j, _):
            @pl.when(k == 0)
            def _():
                wd_copy(j).wait()

                @pl.when(j + 2 < n_dn)
                def _():
                    wd_copy(j + 2).start()

            term = jnp.dot(hbuf[...], wdbuf[j], preferred_element_type=F32)
            sp[j] = term[HALF:].astype(BF16)
            keep[j] = term[:HALF]
            pair_copy(j).start()

            @pl.when((j == 2) | (j == 5))
            def _():
                tick(k * n_dn + (j - 2) // 3)

            return 0

        lax.fori_loop(0, n_dn, down, 0)
        return 0

    lax.fori_loop(0, n_chunks, chunk, 0)

    def last(n, _):
        tick(n)
        return 0

    lax.fori_loop((n_chunks - 1) * n_dn + 2, n_units + 8, last, 0)
    half_y = y_hbm.at[pl.ds(0, y_hbm.shape[0] // 2)]
    done = remote(half_y, half_y, q_send, q_recv, sib)
    done.wait()


def solution(mesh):
    def step(x, w_gate, w_up, w_down):
        rows, depth = x.shape
        hidden = w_gate.shape[1]
        n_chunks, n_gu, n_dn = rows // M, hidden // TH, depth // W
        dma = pltpu.SemaphoreType.DMA
        y = pl.pallas_call(
            functools.partial(kernel, n_chunks, n_gu, n_dn),
            out_shape=jax.ShapeDtypeStruct((rows, depth), BF16),
            in_specs=[pl.BlockSpec(memory_space=pl.ANY)] * 4,
            out_specs=pl.BlockSpec(memory_space=pl.ANY),
            scratch_shapes=[
                pltpu.VMEM((M, depth), BF16),
                pltpu.VMEM((2, depth, 2 * TH), BF16),
                pltpu.VMEM((M, 2 * TH), F32),
                pltpu.VMEM((M, hidden), BF16),
                pltpu.VMEM((n_dn, hidden, W), BF16),
                pltpu.VMEM((n_dn, HALF, W), F32),
                pltpu.VMEM((n_dn, HALF, W), BF16),
                pltpu.VMEM((n_dn, HALF, W), BF16),
                pltpu.VMEM((4, QUARTER, W), F32),
                pltpu.VMEM((4, QUARTER, W), BF16),
                pltpu.VMEM((4, QUARTER, W), BF16),
                pltpu.VMEM((4, EIGHTH, W), F32),
                pltpu.VMEM((4, EIGHTH, W), BF16),
                pltpu.VMEM((4, EIGHTH, W), BF16),
                pltpu.VMEM((4, EIGHTH, W), BF16),
                dma((2,)), dma((2, 2, 2)), dma((n_dn,)),
                dma((n_dn,)), dma((n_dn,)),
                dma((4,)), dma((4,)),
                dma((4,)), dma((4,)),
                dma((4,)),
                dma((4,)), dma((4,)),
                dma((4,)), dma((8,)),
                dma((4,)), dma((8,)),
                dma, dma,
                pltpu.SemaphoreType.REGULAR,
            ],
            compiler_params=pltpu.CompilerParams(
                collective_id=0, has_side_effects=True, vmem_limit_bytes=67043328
            ),
        )(x, w_gate, w_up, w_down)
        return y

    return jax.shard_map(
        step,
        mesh=mesh,
        in_specs=(P("dp", None), P(None, "tp"), P(None, "tp"), P("tp", None)),
        out_specs=P("dp", None),
        check_vma=False,
    )
```

time: 617 us -> 332 us (0.54)
  waiting for transfers between devices: 344 us -> 0 us
  Pallas kernels: 0 us -> 311 us
  matrix products: 240 us -> 0 us
  between operations: 13.4 us -> 0.01 us
    psum x1 -> x0, waiting for transfers between devices: 344 us -> none  [step(): return lax.psum(term, 'tp')]
    pallas_call x0 -> x1, Pallas kernels: none -> 311 us  [step(): pl.pallas_call(functools.partial(kernel, n_chunks, n_gu, n_dn), out_shape...]
    dot_general x3 -> x0, matrix products: 240 us -> none  [the longest x1 84.3 us: step(): up = jnp.dot(x, w_up, preferred_element_type=jnp.float32)]
  transfers between devices with their start and end apart: 1 -> 0, of which waited for: 1 -> 0; matrix products, arithmetic and copies ran while one was open for 0% -> 0% of each run, Pallas kernels for 0% -> 0%
where the time goes in v1:
time: 332 us
  Pallas kernels  311 us (94%)
  local copies, waits for them, and re-layouts  20.2 us (6%)
    pallas_call x1, Pallas kernels, step(): pl.pallas_call(functools.partial(kernel, n_chunks, n_gu, n_dn), out_shape...  311 us
    unnamed x1, local copies, waits for them, and re-layouts  20.2 us

profile of v1, /device:TPU:0, one launch (start us, length us, event | category | flops | bytes accessed | tf_op | source)
XLA Modules:
  0.0 331.5 jit_solution(515790895577143962)
XLA Ops:
  0.0 311.4 %shard_map.46 = bf16[2048,7168]{1,0:T(8,128)(2,1)} custom-call(bf16[2048,7168]{1,0:T(8,128)(2,1)} %x_hbm.1, bf16[7168,2304]{1,0:T(8,128)(2,1)} %wg_hbm.1, bf16[7168,2304]{1,0:T(8,128)(2,1)} %wu_hbm.1, bf16[2304,7168]{1,0:T(8,128)(2,1)} %wd_hbm.1), custom_call_target="tpu_custom_call" | custom-call | tf_op jit(solution)/shard_map/pallas_call | solution.py:263
  311.4 20.2 %copy.6 = bf16[2048,7168]{1,0:T(8,128)(2,1)} copy(bf16[2048,7168]{1,0:T(8,128)(2,1)} %shard_map.46) | data formatting | bytes 58720256

commit v2 on v1

v2 whole, which is shorter than its diff:
```python
import functools

import jax
import jax.numpy as jnp
from jax import lax
from jax.experimental import pallas as pl
from jax.experimental.pallas import tpu as pltpu
from jax.sharding import PartitionSpec as P

MESH = pl.DeviceIdType.MESH
BF16, F32 = jnp.bfloat16, jnp.float32
M = 256
HALF, QUARTER, EIGHTH = M // 2, M // 4, M // 8
TH = 256
W = 1024
RK = 3
L2, L3, L4, L5 = 2, 4, 6, 8


def kernel(
    n_chunks, n_gu, n_dn,
    x_hbm, wg_hbm, wu_hbm, wd_hbm, y_hbm,
    xbuf, wbuf, acc, hbuf, wdbuf, keep, sp, rp, k1, s1, r1, k2, s2, r2, fin,
    x_sem, w_sem, wd_sem, p_send, p_recv, a_send, a_recv, b_send, b_recv,
    g_send, g1_recv, g_recv, q_send, q_recv,
):
    me = lax.axis_index("tp")
    dx, dy, dc = me // 4, (me // 2) % 2, me % 2
    sib = me + 1 - 2 * dc
    kh = x_hbm.shape[1] // 2
    n_tiles = n_chunks * n_gu
    n_units = n_chunks * n_dn

    def remote(src, dst, send, recv, dev):
        return pltpu.make_async_remote_copy(
            src_ref=src, dst_ref=dst, send_sem=send, recv_sem=recv, device_id={"tp": dev}, device_id_type=MESH
        )

    def w_copies(t, part):
        col = pl.multiple_of((t % n_gu) * TH, TH)
        rows = pl.ds(part * kh, kh)
        slot = t % 2
        return [
            pltpu.make_async_copy(
                src.at[rows, pl.ds(col, TH)], wbuf.at[slot, rows, pl.ds(TH * n, TH)], w_sem.at[slot, part, n]
            )
            for n, src in enumerate((wg_hbm, wu_hbm))
        ]

    def x_copies(k):
        own = pl.multiple_of(k * M + dc * HALF, HALF)
        other = pl.multiple_of(k * M + (1 - dc) * HALF, HALF)
        s = k % 2
        return [
            pltpu.make_async_copy(x_hbm.at[pl.ds(own, HALF)], xbuf.at[s, pl.ds(0, HALF)], x_sem.at[s, 0]),
            pltpu.make_async_copy(x_hbm.at[pl.ds(other, HALF)], xbuf.at[s, pl.ds(HALF, HALF)], x_sem.at[s, 1]),
        ]

    def wd_copy(j):
        return pltpu.make_async_copy(
            wd_hbm.at[:, pl.ds(pl.multiple_of(j * W, W), W)], wdbuf.at[j], wd_sem.at[j]
        )

    def pair_copy(u):
        j = u % RK
        return remote(sp.at[j], rp.at[j], p_send.at[j], p_recv.at[j], sib)

    def place(u):
        e = u % 2
        xa, ya = dx + (1 - e) * (1 - 2 * dx), dy + e * (1 - 2 * dy)
        xb, yb = dx + e * (1 - 2 * dx), dy + (1 - e) * (1 - 2 * dy)
        p, r = dx * (1 - e) + dy * e, dx * e + dy * (1 - e)
        return 4 * xa + 2 * ya + dc, 4 * xb + 2 * yb + dc, p, r

    def block(u, p, r):
        row = pl.multiple_of((u // n_dn) * M + dc * HALF + p * QUARTER + r * EIGHTH, EIGHTH)
        return y_hbm.at[pl.ds(row, EIGHTH), pl.ds(pl.multiple_of((u % n_dn) * W, W), W)]

    def half_block(u):
        row = pl.multiple_of((u // n_dn) * M + dc * HALF, HALF)
        return y_hbm.at[pl.ds(row, HALF), pl.ds(pl.multiple_of((u % n_dn) * W, W), W)]

    def a_copy(u):
        a, _, _, _ = place(u)
        s = u % 4
        return remote(s1.at[s], r1.at[s], a_send.at[s], a_recv.at[s], a)

    def b_copy(u):
        _, b, _, _ = place(u)
        s = u % 4
        return remote(s2.at[s], r2.at[s], b_send.at[s], b_recv.at[s], b)

    def loc_copy(u):
        _, _, p, r = place(u)
        return pltpu.make_async_copy(fin.at[u % 4], block(u, p, r), g_send.at[u % 4])

    def g1_copy(u):
        _, b, p, r = place(u)
        return remote(fin.at[u % 4], block(u, p, r), g_send.at[u % 4], g1_recv.at[u % 8], b)

    def g2_copy(u):
        a, _, p, r = place(u)
        return remote(fin.at[u % 4], block(u, p, r), g_send.at[u % 4], g_recv.at[u % 8], a)

    def g3_copy(u):
        a, _, p, r = place(u)
        blk = block(u, p, 1 - r)
        return remote(blk, blk, g_send.at[u % 4], g_recv.at[u % 8], a)

    def q_copy(u):
        blk = half_block(u)
        return remote(blk, blk, q_send, q_recv, sib)

    def step1(u):
        pair_copy(u).wait()
        s, j = u % 4, u % RK
        _, _, p, _ = place(u)
        mine = pl.ds(pl.multiple_of(p * QUARTER, QUARTER), QUARTER)
        theirs = pl.ds(pl.multiple_of((1 - p) * QUARTER, QUARTER), QUARTER)
        s1[s] = (keep[j, theirs] + rp[j, theirs].astype(F32)).astype(BF16)
        k1[s] = keep[j, mine] + rp[j, mine].astype(F32)

    def step2(u):
        a_copy(u).wait()
        s = u % 4
        _, _, _, r = place(u)
        mine = pl.ds(pl.multiple_of(r * EIGHTH, EIGHTH), EIGHTH)
        theirs = pl.ds(pl.multiple_of((1 - r) * EIGHTH, EIGHTH), EIGHTH)
        s2[s] = (k1[s, theirs] + r1[s, theirs].astype(F32)).astype(BF16)
        k2[s] = k1[s, mine] + r1[s, mine].astype(F32)

    def step3(u):
        b_copy(u).wait()
        s = u % 4
        fin[s] = (k2[s] + r2[s].astype(F32)).astype(BF16)

    def step4(u):
        g1_copy(u).wait_recv()

    def step5(u):
        a, _, p, _ = place(u)
        whole = half_block(u)
        remote(whole, whole, g_send.at[u % 4], g_recv.at[u % 8], a).wait_send()
        row = pl.multiple_of((u // n_dn) * M + dc * HALF + (1 - p) * QUARTER, QUARTER)
        two = y_hbm.at[pl.ds(row, QUARTER), pl.ds(pl.multiple_of((u % n_dn) * W, W), W)]
        remote(two, two, g_send.at[u % 4], g_recv.at[u % 8], a).wait_recv()

    def tick(n):
        u5, u4, u3, u2, u1 = n - L5, n - L4, n - L3, n - L2, n
        steady = (u5 >= 0) & (u1 < n_units)

        @pl.when(steady)
        def _():
            step5(u5)
            step4(u4)
            step3(u3)
            step2(u2)
            step1(u1)
            a_copy(u1).start()
            b_copy(u2).start()
            g1_copy(u3).start()
            g3_copy(u4).start()
            g2_copy(u3).start()
            loc_copy(u3).start()
            q_copy(u5).start()

        @pl.when(jnp.logical_not(steady))
        def _():
            @pl.when((u5 >= 0) & (u5 < n_units))
            def _():
                step5(u5)
                q_copy(u5).start()

            @pl.when((u4 >= 0) & (u4 < n_units))
            def _():
                step4(u4)
                g3_copy(u4).start()

            @pl.when((u3 >= 0) & (u3 < n_units))
            def _():
                step3(u3)
                g1_copy(u3).start()
                g2_copy(u3).start()
                loc_copy(u3).start()

            @pl.when((u2 >= 0) & (u2 < n_units))
            def _():
                step2(u2)
                b_copy(u2).start()

            @pl.when((u1 >= 0) & (u1 < n_units))
            def _():
                step1(u1)
                a_copy(u1).start()

    def start(copies):
        for c in copies:
            c.start()

    def wait(copies):
        for c in copies:
            c.wait()

    def hidden_step(k, i):
        t = k * n_gu + i
        slot, xs = t % 2, k % 2

        def refill(part):
            @pl.when(t + 2 < n_tiles)
            def _():
                start(w_copies(t + 2, part))

        wait(w_copies(t, 0))
        acc[...] = jnp.dot(xbuf[xs, :, :kh], wbuf[slot, :kh], preferred_element_type=F32)
        refill(0)
        wait(w_copies(t, 1))
        gu = acc[...] + jnp.dot(xbuf[xs, :, kh:], wbuf[slot, kh:], preferred_element_type=F32)
        g, up = gu[:, :TH], gu[:, TH:]
        hbuf[xs, :, pl.ds(pl.multiple_of(i * TH, TH), TH)] = (g * jax.nn.sigmoid(g) * up).astype(BF16)
        refill(1)

    def term_step(k, j):
        u = k * n_dn + j
        tick(u - 1)

        @pl.when(k == 0)
        def _():
            wd_copy(j).wait()

            @pl.when(j + 2 < n_dn)
            def _():
                wd_copy(j + 2).start()

        term = jnp.dot(hbuf[k % 2], wdbuf[j], preferred_element_type=F32)
        sp[u % RK] = term[HALF:].astype(BF16)
        keep[u % RK] = term[:HALF]
        pair_copy(u).start()

    start(x_copies(0))
    for t in range(2):
        for part in range(2):
            start(w_copies(t, part))

    barrier = pltpu.get_barrier_semaphore()
    partners = (sib, 4 * (1 - dx) + 2 * dy + dc, 4 * dx + 2 * (1 - dy) + dc)
    for dev in partners:
        pl.semaphore_signal(barrier, inc=1, device_id={"tp": dev}, device_id_type=MESH)
    pl.semaphore_wait(barrier, 3)

    def chunk(k, _):
        wait(x_copies(k))

        @pl.when((k > 0) & (k + 1 < n_chunks))
        def _():
            start(x_copies(k + 1))

        def both(i, _):
            @pl.when((k > 0) & (i % 4 != 3))
            def _():
                term_step(k - 1, i - i // 4)

            hidden_step(k, i)
            return 0

        lax.fori_loop(0, n_gu, both, 0)

        @pl.when(k == 0)
        def _():
            start([wd_copy(0), wd_copy(1)])
            start(x_copies(1))

        return 0

    lax.fori_loop(0, n_chunks, chunk, 0)

    def term_only(j, _):
        term_step(n_chunks - 1, j)
        return 0

    lax.fori_loop(0, n_dn, term_only, 0)

    def last(n, _):
        tick(n)
        return 0

    lax.fori_loop(n_units - 1, n_units + L5, last, 0)
    half_y = y_hbm.at[pl.ds(0, y_hbm.shape[0] // 2)]
    remote(half_y, half_y, q_send, q_recv, sib).wait()


def solution(mesh):
    def step(x, w_gate, w_up, w_down):
        rows, depth = x.shape
        hidden = w_gate.shape[1]
        n_chunks, n_gu, n_dn = rows // M, hidden // TH, depth // W
        dma = pltpu.SemaphoreType.DMA
        y = pl.pallas_call(
            functools.partial(kernel, n_chunks, n_gu, n_dn),
            out_shape=jax.ShapeDtypeStruct((rows, depth), BF16),
            in_specs=[pl.BlockSpec(memory_space=pl.ANY)] * 4,
            out_specs=pl.BlockSpec(memory_space=pl.ANY),
            scratch_shapes=[
                pltpu.VMEM((2, M, depth), BF16),
                pltpu.VMEM((2, depth, 2 * TH), BF16),
                pltpu.VMEM((M, 2 * TH), F32),
                pltpu.VMEM((2, M, hidden), BF16),
                pltpu.VMEM((n_dn, hidden, W), BF16),
                pltpu.VMEM((RK, HALF, W), F32),
                pltpu.VMEM((RK, HALF, W), BF16),
                pltpu.VMEM((RK, HALF, W), BF16),
                pltpu.VMEM((4, QUARTER, W), F32),
                pltpu.VMEM((4, QUARTER, W), BF16),
                pltpu.VMEM((4, QUARTER, W), BF16),
                pltpu.VMEM((4, EIGHTH, W), F32),
                pltpu.VMEM((4, EIGHTH, W), BF16),
                pltpu.VMEM((4, EIGHTH, W), BF16),
                pltpu.VMEM((4, EIGHTH, W), BF16),
                dma((2, 2)), dma((2, 2, 2)), dma((n_dn,)),
                dma((RK,)), dma((RK,)),
                dma((4,)), dma((4,)),
                dma((4,)), dma((4,)),
                dma((4,)), dma((8,)), dma((8,)),
                dma, dma,
            ],
            compiler_params=pltpu.CompilerParams(
                collective_id=0, has_side_effects=True, vmem_limit_bytes=67043328
            ),
        )(x, w_gate, w_up, w_down)
        return y

    return jax.shard_map(
        step,
        mesh=mesh,
        in_specs=(P("dp", None), P(None, "tp"), P(None, "tp"), P("tp", None)),
        out_specs=P("dp", None),
        check_vma=False,
    )
```

time: 332 us -> 319 us (0.961)
  Pallas kernels: 311 us -> 299 us
    pallas_call x1, Pallas kernels: 311 us -> 299 us  [step(): pl.pallas_call(functools.partial(kernel, n_chunks, n_gu, n_dn), out_shape...]
where the time goes in v2:
time: 319 us
  Pallas kernels  299 us (94%)
  local copies, waits for them, and re-layouts  20.2 us (6%)
    pallas_call x1, Pallas kernels, step(): pl.pallas_call(functools.partial(kernel, n_chunks, n_gu, n_dn), out_shape...  299 us
    unnamed x1, local copies, waits for them, and re-layouts  20.2 us

profile of v2, /device:TPU:0, one launch (start us, length us, event | category | flops | bytes accessed | tf_op | source)
XLA Modules:
  0.0 319.3 jit_solution(5725016775069386265)
XLA Ops:
  0.0 299.1 %shard_map.46 = bf16[2048,7168]{1,0:T(8,128)(2,1)} custom-call(bf16[2048,7168]{1,0:T(8,128)(2,1)} %x_hbm.1, bf16[7168,2304]{1,0:T(8,128)(2,1)} %wg_hbm.1, bf16[7168,2304]{1,0:T(8,128)(2,1)} %wu_hbm.1, bf16[2304,7168]{1,0:T(8,128)(2,1)} %wd_hbm.1), custom_call_target="tpu_custom_call" | custom-call | tf_op jit(solution)/shard_map/pallas_call | solution.py:297
  299.2 20.2 %copy.6 = bf16[2048,7168]{1,0:T(8,128)(2,1)} copy(bf16[2048,7168]{1,0:T(8,128)(2,1)} %shard_map.46) | data formatting | bytes 58720256

commit v3 on v2

--- a/solution.py
+++ b/solution.py
@@ -13,7 +13,7 @@
 HALF, QUARTER, EIGHTH = M // 2, M // 4, M // 8
 TH = 256
 W = 1024
-RK = 3
+RK = 4
 L2, L3, L4, L5 = 2, 4, 6, 8
 
 
@@ -31,6 +31,12 @@
     n_tiles = n_chunks * n_gu
     n_units = n_chunks * n_dn
 
+    def chunk_of(u):
+        return lax.div(u * (65536 // n_dn + 1), 65536)
+
+    def column_of(u):
+        return u - chunk_of(u) * n_dn
+
     def remote(src, dst, send, recv, dev):
         return pltpu.make_async_remote_copy(
             src_ref=src, dst_ref=dst, send_sem=send, recv_sem=recv, device_id={"tp": dev}, device_id_type=MESH
@@ -62,50 +68,50 @@
         )
 
     def pair_copy(u):
-        j = u % RK
+        j = lax.rem(u, RK)
         return remote(sp.at[j], rp.at[j], p_send.at[j], p_recv.at[j], sib)
 
     def place(u):
-        e = u % 2
+        e = lax.rem(u, 2)
         xa, ya = dx + (1 - e) * (1 - 2 * dx), dy + e * (1 - 2 * dy)
         xb, yb = dx + e * (1 - 2 * dx), dy + (1 - e) * (1 - 2 * dy)
         p, r = dx * (1 - e) + dy * e, dx * e + dy * (1 - e)
         return 4 * xa + 2 * ya + dc, 4 * xb + 2 * yb + dc, p, r
 
     def block(u, p, r):
-        row = pl.multiple_of((u // n_dn) * M + dc * HALF + p * QUARTER + r * EIGHTH, EIGHTH)
-        return y_hbm.at[pl.ds(row, EIGHTH), pl.ds(pl.multiple_of((u % n_dn) * W, W), W)]
+        row = pl.multiple_of(chunk_of(u) * M + dc * HALF + p * QUARTER + r * EIGHTH, EIGHTH)
+        return y_hbm.at[pl.ds(row, EIGHTH), pl.ds(pl.multiple_of(column_of(u) * W, W), W)]
 
     def half_block(u):
-        row = pl.multiple_of((u // n_dn) * M + dc * HALF, HALF)
-        return y_hbm.at[pl.ds(row, HALF), pl.ds(pl.multiple_of((u % n_dn) * W, W), W)]
+        row = pl.multiple_of(chunk_of(u) * M + dc * HALF, HALF)
+        return y_hbm.at[pl.ds(row, HALF), pl.ds(pl.multiple_of(column_of(u) * W, W), W)]
 
     def a_copy(u):
         a, _, _, _ = place(u)
-        s = u % 4
+        s = lax.rem(u, 4)
         return remote(s1.at[s], r1.at[s], a_send.at[s], a_recv.at[s], a)
 
     def b_copy(u):
         _, b, _, _ = place(u)
-        s = u % 4
+        s = lax.rem(u, 4)
         return remote(s2.at[s], r2.at[s], b_send.at[s], b_recv.at[s], b)
 
     def loc_copy(u):
         _, _, p, r = place(u)
-        return pltpu.make_async_copy(fin.at[u % 4], block(u, p, r), g_send.at[u % 4])
+        return pltpu.make_async_copy(fin.at[lax.rem(u, 4)], block(u, p, r), g_send.at[lax.rem(u, 4)])
 
     def g1_copy(u):
         _, b, p, r = place(u)
-        return remote(fin.at[u % 4], block(u, p, r), g_send.at[u % 4], g1_recv.at[u % 8], b)
+        return remote(fin.at[lax.rem(u, 4)], block(u, p, r), g_send.at[lax.rem(u, 4)], g1_recv.at[lax.rem(u, 8)], b)
 
     def g2_copy(u):
         a, _, p, r = place(u)
-        return remote(fin.at[u % 4], block(u, p, r), g_send.at[u % 4], g_recv.at[u % 8], a)
+        return remote(fin.at[lax.rem(u, 4)], block(u, p, r), g_send.at[lax.rem(u, 4)], g_recv.at[lax.rem(u, 8)], a)
 
     def g3_copy(u):
         a, _, p, r = place(u)
         blk = block(u, p, 1 - r)
-        return remote(blk, blk, g_send.at[u % 4], g_recv.at[u % 8], a)
+        return remote(blk, blk, g_send.at[lax.rem(u, 4)], g_recv.at[lax.rem(u, 8)], a)
 
     def q_copy(u):
         blk = half_block(u)
@@ -113,7 +119,7 @@
 
     def step1(u):
         pair_copy(u).wait()
-        s, j = u % 4, u % RK
+        s, j = lax.rem(u, 4), lax.rem(u, RK)
         _, _, p, _ = place(u)
         mine = pl.ds(pl.multiple_of(p * QUARTER, QUARTER), QUARTER)
         theirs = pl.ds(pl.multiple_of((1 - p) * QUARTER, QUARTER), QUARTER)
@@ -122,7 +128,7 @@
 
     def step2(u):
         a_copy(u).wait()
-        s = u % 4
+        s = lax.rem(u, 4)
         _, _, _, r = place(u)
         mine = pl.ds(pl.multiple_of(r * EIGHTH, EIGHTH), EIGHTH)
         theirs = pl.ds(pl.multiple_of((1 - r) * EIGHTH, EIGHTH), EIGHTH)
@@ -131,7 +137,7 @@
 
     def step3(u):
         b_copy(u).wait()
-        s = u % 4
+        s = lax.rem(u, 4)
         fin[s] = (k2[s] + r2[s].astype(F32)).astype(BF16)
 
     def step4(u):
@@ -140,10 +146,10 @@
     def step5(u):
         a, _, p, _ = place(u)
         whole = half_block(u)
-        remote(whole, whole, g_send.at[u % 4], g_recv.at[u % 8], a).wait_send()
-        row = pl.multiple_of((u // n_dn) * M + dc * HALF + (1 - p) * QUARTER, QUARTER)
-        two = y_hbm.at[pl.ds(row, QUARTER), pl.ds(pl.multiple_of((u % n_dn) * W, W), W)]
-        remote(two, two, g_send.at[u % 4], g_recv.at[u % 8], a).wait_recv()
+        remote(whole, whole, g_send.at[lax.rem(u, 4)], g_recv.at[lax.rem(u, 8)], a).wait_send()
+        row = pl.multiple_of(chunk_of(u) * M + dc * HALF + (1 - p) * QUARTER, QUARTER)
+        two = y_hbm.at[pl.ds(row, QUARTER), pl.ds(pl.multiple_of(column_of(u) * W, W), W)]
+        remote(two, two, g_send.at[lax.rem(u, 4)], g_recv.at[lax.rem(u, 8)], a).wait_recv()
 
     def tick(n):
         u5, u4, u3, u2, u1 = n - L5, n - L4, n - L3, n - L2, n
@@ -232,8 +238,8 @@
                 wd_copy(j + 2).start()
 
         term = jnp.dot(hbuf[k % 2], wdbuf[j], preferred_element_type=F32)
-        sp[u % RK] = term[HALF:].astype(BF16)
-        keep[u % RK] = term[:HALF]
+        sp[lax.rem(u, RK)] = term[HALF:].astype(BF16)
+        keep[lax.rem(u, RK)] = term[:HALF]
         pair_copy(u).start()
 
     start(x_copies(0))
@@ -259,15 +265,19 @@
             def _():
                 term_step(k - 1, i - i // 4)
 
+            @pl.when((k == 0) & (i == n_gu - 3))
+            def _():
+                start(x_copies(1))
+                wd_copy(0).start()
+
+            @pl.when((k == 0) & (i == n_gu - 1))
+            def _():
+                wd_copy(1).start()
+
             hidden_step(k, i)
             return 0
 
         lax.fori_loop(0, n_gu, both, 0)
-
-        @pl.when(k == 0)
-        def _():
-            start([wd_copy(0), wd_copy(1)])
-            start(x_copies(1))
 
         return 0
 

time: 319 us -> 315 us (0.987)
  Pallas kernels: 299 us -> 295 us
    pallas_call x1, Pallas kernels: 299 us -> 295 us  [step(): pl.pallas_call(functools.partial(kernel, n_chunks, n_gu, n_dn), out_shape...]
where the time goes in v3:
time: 315 us
  Pallas kernels  295 us (94%)
  local copies, waits for them, and re-layouts  20.2 us (6%)
    pallas_call x1, Pallas kernels, step(): pl.pallas_call(functools.partial(kernel, n_chunks, n_gu, n_dn), out_shape...  295 us
    unnamed x1, local copies, waits for them, and re-layouts  20.2 us

profile of v3, /device:TPU:0, one launch (start us, length us, event | category | flops | bytes accessed | tf_op | source)
XLA Modules:
  0.0 314.8 jit_solution(16773090452076999404)
XLA Ops:
  0.0 294.6 %shard_map.46 = bf16[2048,7168]{1,0:T(8,128)(2,1)} custom-call(bf16[2048,7168]{1,0:T(8,128)(2,1)} %x_hbm.1, bf16[7168,2304]{1,0:T(8,128)(2,1)} %wg_hbm.1, bf16[7168,2304]{1,0:T(8,128)(2,1)} %wu_hbm.1, bf16[2304,7168]{1,0:T(8,128)(2,1)} %wd_hbm.1), custom_call_target="tpu_custom_call" | custom-call | tf_op jit(solution)/shard_map/pallas_call | solution.py:307
  294.6 20.2 %copy.6 = bf16[2048,7168]{1,0:T(8,128)(2,1)} copy(bf16[2048,7168]{1,0:T(8,128)(2,1)} %shard_map.46) | data formatting | bytes 58720256

commit v4 on v3

--- a/solution.py
+++ b/solution.py
@@ -158,10 +158,10 @@
         @pl.when(steady)
         def _():
             step5(u5)
+            step1(u1)
+            step2(u2)
+            step3(u3)
             step4(u4)
-            step3(u3)
-            step2(u2)
-            step1(u1)
             a_copy(u1).start()
             b_copy(u2).start()
             g1_copy(u3).start()
@@ -261,9 +261,9 @@
             start(x_copies(k + 1))
 
         def both(i, _):
-            @pl.when((k > 0) & (i % 4 != 3))
-            def _():
-                term_step(k - 1, i - i // 4)
+            @pl.when((k > 0) & (i != 4) & (i != 8))
+            def _():
+                term_step(k - 1, i - i // 5)
 
             @pl.when((k == 0) & (i == n_gu - 3))
             def _():

time: 315 us -> 315 us (level)
  no operation moved by 1% of the time
where the time goes in v4:
time: 315 us
  Pallas kernels  295 us (94%)
  local copies, waits for them, and re-layouts  20.2 us (6%)
    pallas_call x1, Pallas kernels, step(): pl.pallas_call(functools.partial(kernel, n_chunks, n_gu, n_dn), out_shape...  295 us
    unnamed x1, local copies, waits for them, and re-layouts  20.2 us

profile of v4, /device:TPU:0, one launch (start us, length us, event | category | flops | bytes accessed | tf_op | source)
XLA Modules:
  0.0 314.8 jit_solution(17657235830807517791)
XLA Ops:
  0.0 294.7 %shard_map.46 = bf16[2048,7168]{1,0:T(8,128)(2,1)} custom-call(bf16[2048,7168]{1,0:T(8,128)(2,1)} %x_hbm.1, bf16[7168,2304]{1,0:T(8,128)(2,1)} %wg_hbm.1, bf16[7168,2304]{1,0:T(8,128)(2,1)} %wu_hbm.1, bf16[2304,7168]{1,0:T(8,128)(2,1)} %wd_hbm.1), custom_call_target="tpu_custom_call" | custom-call | tf_op jit(solution)/shard_map/pallas_call | solution.py:307
  294.7 20.2 %copy.6 = bf16[2048,7168]{1,0:T(8,128)(2,1)} copy(bf16[2048,7168]{1,0:T(8,128)(2,1)} %shard_map.46) | data formatting | bytes 58720256
